TPU v7x, 256 devices: a whole 4x4x8 slice. The times are simulated.
256 devices in a mesh: grp: 8 (over z), sp: 32 (over y, x, core).
Axes of the slice: x: 4, y: 4, z: 8, core: 2. Of those that a mesh axis runs over, the one named last changes fastest.
Arguments:
- tokens: bfloat16 [16384, 2880], P(('grp', 'sp')), may hold values from -36 to 36
- query_weight: bfloat16 [2880, 2048], P(None, 'sp'), may hold values from -0.109375 to 0.109375
- key_value_weight: bfloat16 [2880, 1024], replicated, may hold values from -0.109375 to 0.109375
- block_places: int32 [32], replicated, may hold values from 0 to 31, each once
- sinks: float32 [32], replicated, may hold values from -1 to 5
Outputs:
- attended: bfloat16 [16384, 2048], P(('grp', 'sp'))
Inputs may be any that keep to these rules, and one draw needn't show every extreme that they name: `block_places`: every sequence block appears once.
All inputs are finite; a program needn't handle non-finite values.
Results may differ from a plain program's by a relative error of at most 0.008.
The roundings to bfloat16 on the way count: a program that leaves them out, or rounds other values in their place, can miss the bound.
Values may be sent and summed in bfloat16 or wider, within the bound.
A program may use at most 128 MiB of HBM per device.

v0:
```python
import jax
import jax.numpy as jnp
from jax import lax
from jax.sharding import PartitionSpec as P

QUERY_HEADS = 32
HEAD_SIZE = 64
BPG = 4
rope_base = 150000.0
neg_large = -1e30


def joined_along(pieces, dim):
    pieces = jnp.moveaxis(pieces, 0, dim)
    shape = pieces.shape
    return pieces.reshape(*shape[:dim], shape[dim] * shape[dim + 1], *shape[dim + 2 :])


def piecewise(value, axis, dim, apply, out_dim):
    size, span = (lax.axis_size(axis), value.shape[dim])
    count = 2 if span % 2 == 0 else 1
    finished, length = ([], span // count)
    for k in range(count):
        share = lax.slice_in_dim(value, k * length, (k + 1) * length, axis=dim)
        starts = jnp.arange(size) * span + k * length
        finished.append(jax.vmap(apply)(lax.all_gather(share, axis), starts))
    return joined_along(jnp.concatenate(finished, axis=out_dim + 1), out_dim)


def rotate(vectors, angles):
    middle = vectors.shape[-1] // 2
    first_half = vectors[..., :middle]
    second_half = vectors[..., middle:]
    cosine = jnp.cos(angles)
    sine_part = jnp.sin(angles)
    return jnp.concatenate(
        [
            first_half * cosine - second_half * sine_part,
            second_half * cosine + first_half * sine_part,
        ],
        axis=-1,
    )


def locate(stored, block_rows, block_places):
    blocks = stored // block_rows
    table = jnp.arange(block_places.shape[0], dtype=jnp.int32)
    onehot = (blocks[:, None] == table[None, :]).astype(jnp.int32)
    return jnp.sum(onehot * block_places[None, :], axis=1) * block_rows + stored % block_rows


def prepare(projected, own_places, query_cols, kv_cols, head_count):
    row_count = projected.shape[0]
    inverse = rope_base ** (-(jnp.arange(HEAD_SIZE // 2, dtype=jnp.float32) * 2.0) / HEAD_SIZE)
    angles = own_places.astype(jnp.float32)[:, None, None] * inverse[None, None, :]
    queries = rotate(
        projected[:, :query_cols].reshape(row_count, query_cols // HEAD_SIZE, HEAD_SIZE), angles
    ).astype(jnp.bfloat16)
    rotated_keys = rotate(
        projected[:, query_cols : query_cols + kv_cols].reshape(row_count, head_count, HEAD_SIZE),
        angles,
    )
    key_value_pair = jnp.concatenate(
        [rotated_keys.reshape(row_count, kv_cols), projected[:, query_cols + kv_cols :]], axis=1
    ).astype(jnp.bfloat16)
    return (queries, key_value_pair)


def attend(state, queries, query_places, key_value_pair, key_places, head_count):
    maxima, totals, mixture = state
    key_count = key_value_pair.shape[0]
    column_half = key_value_pair.shape[1] // 2
    key_part = key_value_pair[:, :column_half].reshape(key_count, head_count, HEAD_SIZE)
    value_part = key_value_pair[:, column_half:].reshape(key_count, head_count, HEAD_SIZE)
    scores = jnp.einsum(
        "qhgd,khd->hgqk", queries, key_part, preferred_element_type=jnp.float32
    ) * HEAD_SIZE ** (-0.5)
    allowed = key_places[None, :] <= query_places[:, None]
    scores = jnp.where(allowed, scores, neg_large)
    updated = jnp.maximum(maxima, jnp.max(scores, axis=-1))
    weights = jnp.where(allowed, jnp.exp(scores - updated[..., None]), 0.0)
    factor = jnp.exp(maxima - updated)
    totals = totals * factor + jnp.sum(weights, axis=-1)
    mixture = mixture * factor[..., None] + jnp.einsum(
        "hgqk,khd->hgqd",
        weights.astype(jnp.bfloat16),
        value_part,
        preferred_element_type=jnp.float32,
    )
    return (updated, totals, mixture)


def per_device(tokens, query_weight, key_value_weight, block_places, sinks):
    sp_count = lax.axis_size("sp")
    local_rows = tokens.shape[0]
    group_rows = local_rows * sp_count
    block_rows = group_rows // BPG
    kv_total = key_value_weight.shape[1] // (2 * HEAD_SIZE)
    sp_place = lax.axis_index("sp")
    grp_place = lax.axis_index("grp")
    query_cols = query_weight.shape[1]
    query_heads = query_cols // HEAD_SIZE
    head_count = max(kv_total // sp_count, 1)
    kv_cols = head_count * HEAD_SIZE
    first_head = sp_place * query_heads // (QUERY_HEADS // kv_total)
    key_weight = lax.dynamic_slice_in_dim(key_value_weight, first_head * HEAD_SIZE, kv_cols, 1)
    value_weight = lax.dynamic_slice_in_dim(
        key_value_weight, kv_total * HEAD_SIZE + first_head * HEAD_SIZE, kv_cols, 1
    )
    joined = jnp.concatenate([query_weight, key_weight, value_weight], axis=1)

    def project(piece, start):
        return jnp.dot(piece, joined, preferred_element_type=jnp.float32)

    projected = piecewise(tokens, "sp", 0, project, 0)
    query_local = jnp.arange(group_rows, dtype=jnp.int32)
    head_first = sp_place * query_heads
    own_places = locate(grp_place * group_rows + query_local, block_rows, block_places)
    queries, key_value_pair = prepare(projected, own_places, query_cols, kv_cols, head_count)
    query_sharing = query_heads // head_count
    head_sinks = lax.dynamic_slice_in_dim(sinks, head_first, query_heads, 0).reshape(
        head_count, query_sharing
    )
    sink_rows = jnp.broadcast_to(head_sinks[:, :, None], (head_count, query_sharing, group_rows))
    query_block4 = queries.reshape(group_rows, head_count, query_sharing, HEAD_SIZE)
    initial = (
        sink_rows,
        jnp.ones((head_count, query_sharing, group_rows), jnp.float32),
        jnp.zeros((head_count, query_sharing, group_rows, HEAD_SIZE), jnp.float32),
    )
    piece = lax.all_gather(key_value_pair, "grp", axis=0, tiled=True)
    step_rows = min(piece.shape[0], group_rows)
    turns = piece.shape[0] // step_rows

    def visit(turn, inner):
        offset = turn * step_rows
        piece_rows = lax.dynamic_slice_in_dim(piece, offset, step_rows, 0)
        position = offset + jnp.arange(step_rows, dtype=jnp.int32)
        stored = position // group_rows * group_rows + position % group_rows
        key_places = locate(stored, block_rows, block_places)
        return attend(inner, query_block4, own_places, piece_rows, key_places, head_count)

    maxima, totals, mixture = lax.fori_loop(0, turns, visit, initial)
    normed = jnp.transpose(mixture, (2, 0, 1, 3)) / jnp.transpose(totals, (2, 0, 1))[..., None]
    attended = normed.reshape(group_rows, query_cols).astype(jnp.bfloat16)
    return lax.all_to_all(attended, "sp", split_axis=0, concat_axis=1, tiled=True)


def solution(mesh):
    in_specs = (P(("grp", "sp"), None), P(None, "sp"), P(), P(), P())
    out_specs = P(("grp", "sp"), None)
    return jax.shard_map(
        per_device, mesh=mesh, in_specs=in_specs, out_specs=out_specs, check_vma=False
    )
```

profile of v0, /device:TPU:1, one launch (start us, length us, event | category | flops | bytes accessed | tf_op | source)
XLA Modules:
  0.0 353.2 jit_solution(3869679549317436455)
XLA Ops:
  6.5 1.8 fusion.61
  8.4 0.7 all-gather.10.cloned.1.call-update
  9.2 1.8 constant_dynamic-slice_fusion.1
  11.0 0.3 copy.43
  11.3 0.3 copy.44
  11.7 0.1 select_reduce_fusion.1
  11.8 55.8 %all-gather.8.cloned.1.call-done = bf16[1024,2880]{1,0:T(8,128)(2,1)} async-done(((bf16[32,2880]{1,0:T(8,128)(2,1)}), bf16[1024,2880]{1,0:T(8,128)(2,1)}) %all-gather.8.cloned.1.call-update) | async-done | bytes 5898256 | tf_op jit(solution)/shard_map/all_gather | solution.py:26
  67.6 4.5 %convolution_bitcast_fusion.1 = f32[32,32,192]{2,1,0:T(8,128)S(1)} fusion(bf16[32,32,2880]{2,1,0:T(8,128)(2,1)} %bitcast.94, bf16[2880,64]{0,1:T(8,128)(2,1)S(1)} %copy.44, bf16[2880,64]{0,1:T(8,128)(2,1)S(1)} %copy.43, bf16[2880,64]{0,1:T(8,128)(2,1)S(1)} %copy-done.2), kind=kOutput, calls=%fused_computation.49 | convolution fusion | flops 1135779840 | bytes 7790592 | tf_op jit(solution)/shard_map/vmap()/dot_general | solution.py:113
  72.1 50.5 %all-gather.10.cloned.1.call-done = bf16[1024,2880]{1,0:T(8,128)(2,1)} async-done(((bf16[32,2880]{1,0:T(8,128)(2,1)}), bf16[1024,2880]{1,0:T(8,128)(2,1)}) %all-gather.10.cloned.1.call-update) | async-done | bytes 5898256 | tf_op jit(solution)/shard_map/all_gather | solution.py:26
  122.6 4.5 %convolution_bitcast_fusion = f32[32,32,192]{2,1,0:T(8,128)S(1)} fusion(bf16[32,32,2880]{2,1,0:T(8,128)(2,1)} %bitcast.95, bf16[2880,64]{0,1:T(8,128)(2,1)S(1)} %copy.44, bf16[2880,64]{0,1:T(8,128)(2,1)S(1)} %copy.43, bf16[2880,64]{0,1:T(8,128)(2,1)S(1)} %copy-done.2), kind=kOutput, calls=%fused_computation.48 | convolution fusion | flops 1135779840 | bytes 7790592 | tf_op jit(solution)/shard_map/vmap()/dot_general | solution.py:113
  127.1 0.2 pad_maximum_fusion
  127.3 0.3 fusion.60
  127.8 0.3 copy.47
  128.1 0.3 copy.49
  128.4 0.2 copy.48
  128.6 1.2 fusion.49
  129.9 0.8 pad_maximum_fusion.1
  130.7 0.6 dynamic_slice.20
  131.3 52.6 %all-gather.6.cloned.1.call-done = bf16[16384,128]{0,1:T(8,128)(2,1)} async-done(((bf16[2048,128]{0,1:T(8,128)(2,1)}), bf16[16384,128]{0,1:T(8,128)(2,1)}) %all-gather.6.cloned.1.call-update) | async-done | bytes 4194320 | tf_op jit(solution)/shard_map/all_gather | solution.py:131
  183.9 0.6 broadcast_in_dim.68
  184.5 141.5 %while.21 = (s32[]{:T(128)}, f32[1,1,2048]{2,1,0:T(1,128)S(1)}, f32[1,1,2048]{2,1,0:T(1,128)S(1)}, f32[1,1,2048,64]{2,3,1,0:T(8,128)S(1)}, s32[32]{0:T(128)S(1)}...) while((s32[]{:T(128)}, f32[1,1,2048]{2,1,0:T(1,128)S(1)}, ...), condition=%wide.region_5.6_spmd.clone, body=%wide.region_1.5_spmd.clone.sunk | while | flops 1141592064 | bytes 119497064 | solution.py:143
  184.6 0.1 select_reduce_fusion.3
  184.7 3.6 %fusion.74 = (f32[2048]{0:T(1024)S(1)}, f32[2048,2048]{1,0:T(8,128)S(1)}) fusion(s32[2048]{0:T(1024)S(1)} %get-tuple-element.427, s32[2048]{0:T(1024)S(1)} %fusion.73, bf16[2048,1,1,64]{0,3,2,1:T(8,128)(2,1)S(1)} %get-tuple-element.429, bf16[16384,128]{0,1:T(8,128)(2,1)} %get-tuple-element.428, s32[]{:T(128)S(6)} %select_n.248), kind=kOutput, calls=%fused_computation.2.clone.1 | convolution fusion | flops 553646080 | bytes 17326084 | tf_op jit(solution)/shard_map/while/body/eval_jaxpr/qhgd,khd->hgqk/dot_general | solution.py:75
  188.3 5.3 %fusion.75 = f32[2048]{0:T(1024)S(1)} fusion(f32[2048,2048]{1,0:T(8,128)S(1)} %get-tuple-element.393, f32[2048]{0:T(1024)S(1)} %bitcast.86, s32[2048]{0:T(1024)S(1)} %get-tuple-element.427, s32[2048]{0:T(1024)S(1)} %fusion.73), kind=kLoop, calls=%fused_computation.4.clone.1 | loop fusion | flops 25163776 | bytes 16809984 | tf_op jit(solution)/shard_map/while/body/eval_jaxpr/reduce_sum | solution.py:83
  193.6 0.4 copy-done
  194.1 8.1 %fusion.77 = f32[1,1,2048,64]{2,3,1,0:T(8,128)S(1)} fusion(f32[2048,2048]{1,0:T(8,128)} %copy-done, f32[2048]{0:T(1024)S(1)} %bitcast.87, s32[2048]{0:T(1024)S(1)} %get-tuple-element.427, s32[2048]{0:T(1024)S(1)} %fusion.73, f32[1,1,2048,64]{2,3,1,0:T(8,128)S(1)} %get-tuple-element.412, bf16[16384,128]{0,1:T(8,128)(2,1)} %get-tuple-element.428, ...), kind=kOutput, calls=%fused_computation.8.clone.1 | convolution fusion | flops 562429952 | bytes 18120712 | tf_op jit(solution)/shard_map/while/body/eval_jaxpr/hgqk,khd->hgqd/dot_general | solution.py:84
  202.4 3.6 %fusion.74 = (f32[2048]{0:T(1024)S(1)}, f32[2048,2048]{1,0:T(8,128)S(1)}) fusion(s32[2048]{0:T(1024)S(1)} %get-tuple-element.427, s32[2048]{0:T(1024)S(1)} %fusion.73, bf16[2048,1,1,64]{0,3,2,1:T(8,128)(2,1)S(1)} %get-tuple-element.429, bf16[16384,128]{0,1:T(8,128)(2,1)} %get-tuple-element.428, s32[]{:T(128)S(6)} %select_n.248), kind=kOutput, calls=%fused_computation.2.clone.1 | convolution fusion | flops 553646080 | bytes 17326084 | tf_op jit(solution)/shard_map/while/body/eval_jaxpr/qhgd,khd->hgqk/dot_general | solution.py:75
  206.0 5.3 %fusion.75 = f32[2048]{0:T(1024)S(1)} fusion(f32[2048,2048]{1,0:T(8,128)S(1)} %get-tuple-element.393, f32[2048]{0:T(1024)S(1)} %bitcast.86, s32[2048]{0:T(1024)S(1)} %get-tuple-element.427, s32[2048]{0:T(1024)S(1)} %fusion.73), kind=kLoop, calls=%fused_computation.4.clone.1 | loop fusion | flops 25163776 | bytes 16809984 | tf_op jit(solution)/shard_map/while/body/eval_jaxpr/reduce_sum | solution.py:83
  211.3 0.4 copy-done
  211.8 8.1 %fusion.77 = f32[1,1,2048,64]{2,3,1,0:T(8,128)S(1)} fusion(f32[2048,2048]{1,0:T(8,128)} %copy-done, f32[2048]{0:T(1024)S(1)} %bitcast.87, s32[2048]{0:T(1024)S(1)} %get-tuple-element.427, s32[2048]{0:T(1024)S(1)} %fusion.73, f32[1,1,2048,64]{2,3,1,0:T(8,128)S(1)} %get-tuple-element.412, bf16[16384,128]{0,1:T(8,128)(2,1)} %get-tuple-element.428, ...), kind=kOutput, calls=%fused_computation.8.clone.1 | convolution fusion | flops 562429952 | bytes 18120712 | tf_op jit(solution)/shard_map/while/body/eval_jaxpr/hgqk,khd->hgqd/dot_general | solution.py:84
  220.0 0.1 select_reduce_fusion.3
  220.1 3.6 %fusion.74 = (f32[2048]{0:T(1024)S(1)}, f32[2048,2048]{1,0:T(8,128)S(1)}) fusion(s32[2048]{0:T(1024)S(1)} %get-tuple-element.427, s32[2048]{0:T(1024)S(1)} %fusion.73, bf16[2048,1,1,64]{0,3,2,1:T(8,128)(2,1)S(1)} %get-tuple-element.429, bf16[16384,128]{0,1:T(8,128)(2,1)} %get-tuple-element.428, s32[]{:T(128)S(6)} %select_n.248), kind=kOutput, calls=%fused_computation.2.clone.1 | convolution fusion | flops 553646080 | bytes 17326084 | tf_op jit(solution)/shard_map/while/body/eval_jaxpr/qhgd,khd->hgqk/dot_general | solution.py:75
  223.7 5.3 %fusion.75 = f32[2048]{0:T(1024)S(1)} fusion(f32[2048,2048]{1,0:T(8,128)S(1)} %get-tuple-element.393, f32[2048]{0:T(1024)S(1)} %bitcast.86, s32[2048]{0:T(1024)S(1)} %get-tuple-element.427, s32[2048]{0:T(1024)S(1)} %fusion.73), kind=kLoop, calls=%fused_computation.4.clone.1 | loop fusion | flops 25163776 | bytes 16809984 | tf_op jit(solution)/shard_map/while/body/eval_jaxpr/reduce_sum | solution.py:83
  229.0 0.4 copy-done
  229.5 8.1 %fusion.77 = f32[1,1,2048,64]{2,3,1,0:T(8,128)S(1)} fusion(f32[2048,2048]{1,0:T(8,128)} %copy-done, f32[2048]{0:T(1024)S(1)} %bitcast.87, s32[2048]{0:T(1024)S(1)} %get-tuple-element.427, s32[2048]{0:T(1024)S(1)} %fusion.73, f32[1,1,2048,64]{2,3,1,0:T(8,128)S(1)} %get-tuple-element.412, bf16[16384,128]{0,1:T(8,128)(2,1)} %get-tuple-element.428, ...), kind=kOutput, calls=%fused_computation.8.clone.1 | convolution fusion | flops 562429952 | bytes 18120712 | tf_op jit(solution)/shard_map/while/body/eval_jaxpr/hgqk,khd->hgqd/dot_general | solution.py:84
  237.8 3.6 %fusion.74 = (f32[2048]{0:T(1024)S(1)}, f32[2048,2048]{1,0:T(8,128)S(1)}) fusion(s32[2048]{0:T(1024)S(1)} %get-tuple-element.427, s32[2048]{0:T(1024)S(1)} %fusion.73, bf16[2048,1,1,64]{0,3,2,1:T(8,128)(2,1)S(1)} %get-tuple-element.429, bf16[16384,128]{0,1:T(8,128)(2,1)} %get-tuple-element.428, s32[]{:T(128)S(6)} %select_n.248), kind=kOutput, calls=%fused_computation.2.clone.1 | convolution fusion | flops 553646080 | bytes 17326084 | tf_op jit(solution)/shard_map/while/body/eval_jaxpr/qhgd,khd->hgqk/dot_general | solution.py:75
  241.4 5.3 %fusion.75 = f32[2048]{0:T(1024)S(1)} fusion(f32[2048,2048]{1,0:T(8,128)S(1)} %get-tuple-element.393, f32[2048]{0:T(1024)S(1)} %bitcast.86, s32[2048]{0:T(1024)S(1)} %get-tuple-element.427, s32[2048]{0:T(1024)S(1)} %fusion.73), kind=kLoop, calls=%fused_computation.4.clone.1 | loop fusion | flops 25163776 | bytes 16809984 | tf_op jit(solution)/shard_map/while/body/eval_jaxpr/reduce_sum | solution.py:83
  246.7 0.4 copy-done
  247.1 8.1 %fusion.77 = f32[1,1,2048,64]{2,3,1,0:T(8,128)S(1)} fusion(f32[2048,2048]{1,0:T(8,128)} %copy-done, f32[2048]{0:T(1024)S(1)} %bitcast.87, s32[2048]{0:T(1024)S(1)} %get-tuple-element.427, s32[2048]{0:T(1024)S(1)} %fusion.73, f32[1,1,2048,64]{2,3,1,0:T(8,128)S(1)} %get-tuple-element.412, bf16[16384,128]{0,1:T(8,128)(2,1)} %get-tuple-element.428, ...), kind=kOutput, calls=%fused_computation.8.clone.1 | convolution fusion | flops 562429952 | bytes 18120712 | tf_op jit(solution)/shard_map/while/body/eval_jaxpr/hgqk,khd->hgqd/dot_general | solution.py:84
  255.5 3.6 %fusion.74 = (f32[2048]{0:T(1024)S(1)}, f32[2048,2048]{1,0:T(8,128)S(1)}) fusion(s32[2048]{0:T(1024)S(1)} %get-tuple-element.427, s32[2048]{0:T(1024)S(1)} %fusion.73, bf16[2048,1,1,64]{0,3,2,1:T(8,128)(2,1)S(1)} %get-tuple-element.429, bf16[16384,128]{0,1:T(8,128)(2,1)} %get-tuple-element.428, s32[]{:T(128)S(6)} %select_n.248), kind=kOutput, calls=%fused_computation.2.clone.1 | convolution fusion | flops 553646080 | bytes 17326084 | tf_op jit(solution)/shard_map/while/body/eval_jaxpr/qhgd,khd->hgqk/dot_general | solution.py:75
  259.1 5.3 %fusion.75 = f32[2048]{0:T(1024)S(1)} fusion(f32[2048,2048]{1,0:T(8,128)S(1)} %get-tuple-element.393, f32[2048]{0:T(1024)S(1)} %bitcast.86, s32[2048]{0:T(1024)S(1)} %get-tuple-element.427, s32[2048]{0:T(1024)S(1)} %fusion.73), kind=kLoop, calls=%fused_computation.4.clone.1 | loop fusion | flops 25163776 | bytes 16809984 | tf_op jit(solution)/shard_map/while/body/eval_jaxpr/reduce_sum | solution.py:83
  264.4 0.4 copy-done
  264.8 8.1 %fusion.77 = f32[1,1,2048,64]{2,3,1,0:T(8,128)S(1)} fusion(f32[2048,2048]{1,0:T(8,128)} %copy-done, f32[2048]{0:T(1024)S(1)} %bitcast.87, s32[2048]{0:T(1024)S(1)} %get-tuple-element.427, s32[2048]{0:T(1024)S(1)} %fusion.73, f32[1,1,2048,64]{2,3,1,0:T(8,128)S(1)} %get-tuple-element.412, bf16[16384,128]{0,1:T(8,128)(2,1)} %get-tuple-element.428, ...), kind=kOutput, calls=%fused_computation.8.clone.1 | convolution fusion | flops 562429952 | bytes 18120712 | tf_op jit(solution)/shard_map/while/body/eval_jaxpr/hgqk,khd->hgqd/dot_general | solution.py:84
  273.2 3.6 %fusion.74 = (f32[2048]{0:T(1024)S(1)}, f32[2048,2048]{1,0:T(8,128)S(1)}) fusion(s32[2048]{0:T(1024)S(1)} %get-tuple-element.427, s32[2048]{0:T(1024)S(1)} %fusion.73, bf16[2048,1,1,64]{0,3,2,1:T(8,128)(2,1)S(1)} %get-tuple-element.429, bf16[16384,128]{0,1:T(8,128)(2,1)} %get-tuple-element.428, s32[]{:T(128)S(6)} %select_n.248), kind=kOutput, calls=%fused_computation.2.clone.1 | convolution fusion | flops 553646080 | bytes 17326084 | tf_op jit(solution)/shard_map/while/body/eval_jaxpr/qhgd,khd->hgqk/dot_general | solution.py:75
  276.8 5.3 %fusion.75 = f32[2048]{0:T(1024)S(1)} fusion(f32[2048,2048]{1,0:T(8,128)S(1)} %get-tuple-element.393, f32[2048]{0:T(1024)S(1)} %bitcast.86, s32[2048]{0:T(1024)S(1)} %get-tuple-element.427, s32[2048]{0:T(1024)S(1)} %fusion.73), kind=kLoop, calls=%fused_computation.4.clone.1 | loop fusion | flops 25163776 | bytes 16809984 | tf_op jit(solution)/shard_map/while/body/eval_jaxpr/reduce_sum | solution.py:83
  282.1 0.4 copy-done
  282.5 8.1 %fusion.77 = f32[1,1,2048,64]{2,3,1,0:T(8,128)S(1)} fusion(f32[2048,2048]{1,0:T(8,128)} %copy-done, f32[2048]{0:T(1024)S(1)} %bitcast.87, s32[2048]{0:T(1024)S(1)} %get-tuple-element.427, s32[2048]{0:T(1024)S(1)} %fusion.73, f32[1,1,2048,64]{2,3,1,0:T(8,128)S(1)} %get-tuple-element.412, bf16[16384,128]{0,1:T(8,128)(2,1)} %get-tuple-element.428, ...), kind=kOutput, calls=%fused_computation.8.clone.1 | convolution fusion | flops 562429952 | bytes 18120712 | tf_op jit(solution)/shard_map/while/body/eval_jaxpr/hgqk,khd->hgqd/dot_general | solution.py:84
  290.9 3.6 %fusion.74 = (f32[2048]{0:T(1024)S(1)}, f32[2048,2048]{1,0:T(8,128)S(1)}) fusion(s32[2048]{0:T(1024)S(1)} %get-tuple-element.427, s32[2048]{0:T(1024)S(1)} %fusion.73, bf16[2048,1,1,64]{0,3,2,1:T(8,128)(2,1)S(1)} %get-tuple-element.429, bf16[16384,128]{0,1:T(8,128)(2,1)} %get-tuple-element.428, s32[]{:T(128)S(6)} %select_n.248), kind=kOutput, calls=%fused_computation.2.clone.1 | convolution fusion | flops 553646080 | bytes 17326084 | tf_op jit(solution)/shard_map/while/body/eval_jaxpr/qhgd,khd->hgqk/dot_general | solution.py:75
  294.5 5.3 %fusion.75 = f32[2048]{0:T(1024)S(1)} fusion(f32[2048,2048]{1,0:T(8,128)S(1)} %get-tuple-element.393, f32[2048]{0:T(1024)S(1)} %bitcast.86, s32[2048]{0:T(1024)S(1)} %get-tuple-element.427, s32[2048]{0:T(1024)S(1)} %fusion.73), kind=kLoop, calls=%fused_computation.4.clone.1 | loop fusion | flops 25163776 | bytes 16809984 | tf_op jit(solution)/shard_map/while/body/eval_jaxpr/reduce_sum | solution.py:83
  299.8 0.4 copy-done
  300.2 8.1 %fusion.77 = f32[1,1,2048,64]{2,3,1,0:T(8,128)S(1)} fusion(f32[2048,2048]{1,0:T(8,128)} %copy-done, f32[2048]{0:T(1024)S(1)} %bitcast.87, s32[2048]{0:T(1024)S(1)} %get-tuple-element.427, s32[2048]{0:T(1024)S(1)} %fusion.73, f32[1,1,2048,64]{2,3,1,0:T(8,128)S(1)} %get-tuple-element.412, bf16[16384,128]{0,1:T(8,128)(2,1)} %get-tuple-element.428, ...), kind=kOutput, calls=%fused_computation.8.clone.1 | convolution fusion | flops 562429952 | bytes 18120712 | tf_op jit(solution)/shard_map/while/body/eval_jaxpr/hgqk,khd->hgqd/dot_general | solution.py:84
  308.6 3.6 %fusion.74 = (f32[2048]{0:T(1024)S(1)}, f32[2048,2048]{1,0:T(8,128)S(1)}) fusion(s32[2048]{0:T(1024)S(1)} %get-tuple-element.427, s32[2048]{0:T(1024)S(1)} %fusion.73, bf16[2048,1,1,64]{0,3,2,1:T(8,128)(2,1)S(1)} %get-tuple-element.429, bf16[16384,128]{0,1:T(8,128)(2,1)} %get-tuple-element.428, s32[]{:T(128)S(6)} %select_n.248), kind=kOutput, calls=%fused_computation.2.clone.1 | convolution fusion | flops 553646080 | bytes 17326084 | tf_op jit(solution)/shard_map/while/body/eval_jaxpr/qhgd,khd->hgqk/dot_general | solution.py:75
  312.2 5.3 %fusion.75 = f32[2048]{0:T(1024)S(1)} fusion(f32[2048,2048]{1,0:T(8,128)S(1)} %get-tuple-element.393, f32[2048]{0:T(1024)S(1)} %bitcast.86, s32[2048]{0:T(1024)S(1)} %get-tuple-element.427, s32[2048]{0:T(1024)S(1)} %fusion.73), kind=kLoop, calls=%fused_computation.4.clone.1 | loop fusion | flops 25163776 | bytes 16809984 | tf_op jit(solution)/shard_map/while/body/eval_jaxpr/reduce_sum | solution.py:83
  317.5 0.4 copy-done
  317.9 8.1 %fusion.77 = f32[1,1,2048,64]{2,3,1,0:T(8,128)S(1)} fusion(f32[2048,2048]{1,0:T(8,128)} %copy-done, f32[2048]{0:T(1024)S(1)} %bitcast.87, s32[2048]{0:T(1024)S(1)} %get-tuple-element.427, s32[2048]{0:T(1024)S(1)} %fusion.73, f32[1,1,2048,64]{2,3,1,0:T(8,128)S(1)} %get-tuple-element.412, bf16[16384,128]{0,1:T(8,128)(2,1)} %get-tuple-element.428, ...), kind=kOutput, calls=%fused_computation.8.clone.1 | convolution fusion | flops 562429952 | bytes 18120712 | tf_op jit(solution)/shard_map/while/body/eval_jaxpr/hgqk,khd->hgqd/dot_general | solution.py:84
  326.1 0.3 copy.40
  326.4 0.5 broadcast.645
  326.9 0.7 reduce.17
  327.7 0.3 divide_convert_fusion
  328.0 0.4 reshape.437
  328.4 16.4 %all_to_all.16 = bf16[32,2,2048]{2,1,0:T(2,128)(2,1)S(1)} all-to-all(bf16[32,2,2048]{2,1,0:T(2,128)(2,1)S(1)} %reshape.437), channel_id=1, replica_groups=mesh['grp'=8,'sp'=32] {'sp'}, dimensions={0} | all-to-all | bytes 524288 | tf_op jit(solution)/shard_map/all_to_all | solution.py:146
  344.8 0.4 reshape.438
  345.1 0.3 copy.41
  345.5 1.2 all_to_all.14
  (74 shorter events, 1.8 us)
Async XLA Ops:
  6.5 5.1 %copy-start.1 = (s32[32]{0:T(128)S(1)}, s32[32]{0:T(128)}, u32[]{:S(2)}) copy-start(s32[32]{0:T(128)} %param.10) | copy-start | bytes 388
  6.5 61.1 %copy-start.2 = (bf16[2880,64]{0,1:T(8,128)(2,1)S(1)}, bf16[2880,64]{0,1:T(8,128)(2,1)}, u32[]{:S(2)}) copy-start(bf16[2880,64]{0,1:T(8,128)(2,1)} %param.8) | copy-start | bytes 1105924
  6.5 61.1 %all-gather.8.cloned.1.call-start = ((), (), s32[]{:S(2)}) async-start(), calls=%async_computation.2 | async-start | bytes 6217728 | tf_op jit(solution)/shard_map/all_gather | solution.py:26
  8.4 114.2 %all-gather.10.cloned.1.call-start = ((), (), s32[]{:S(2)}) async-start(), calls=%async_computation.3 | async-start | bytes 6217728 | tf_op jit(solution)/shard_map/all_gather | solution.py:26
  9.1 174.8 %all-gather.6.cloned.1.call-start = ((), (), s32[]{:S(2)}) async-start(), calls=%async_computation.1 | async-start | bytes 4718592 | tf_op jit(solution)/shard_map/all_gather | solution.py:131
  127.3 3.4 copy-start.3
  188.3 5.7 %copy-start = (f32[2048,2048]{1,0:T(8,128)}, f32[2048,2048]{1,0:T(8,128)S(1)}, u32[]{:S(2)}) copy-start(f32[2048,2048]{1,0:T(8,128)S(1)} %get-tuple-element.393) | copy-start | bytes 50331652 | tf_op jit(solution)/shard_map/while
  206.0 5.7 %copy-start = (f32[2048,2048]{1,0:T(8,128)}, f32[2048,2048]{1,0:T(8,128)S(1)}, u32[]{:S(2)}) copy-start(f32[2048,2048]{1,0:T(8,128)S(1)} %get-tuple-element.393) | copy-start | bytes 50331652 | tf_op jit(solution)/shard_map/while
  223.7 5.7 %copy-start = (f32[2048,2048]{1,0:T(8,128)}, f32[2048,2048]{1,0:T(8,128)S(1)}, u32[]{:S(2)}) copy-start(f32[2048,2048]{1,0:T(8,128)S(1)} %get-tuple-element.393) | copy-start | bytes 50331652 | tf_op jit(solution)/shard_map/while
  241.4 5.7 %copy-start = (f32[2048,2048]{1,0:T(8,128)}, f32[2048,2048]{1,0:T(8,128)S(1)}, u32[]{:S(2)}) copy-start(f32[2048,2048]{1,0:T(8,128)S(1)} %get-tuple-element.393) | copy-start | bytes 50331652 | tf_op jit(solution)/shard_map/while
  259.1 5.7 %copy-start = (f32[2048,2048]{1,0:T(8,128)}, f32[2048,2048]{1,0:T(8,128)S(1)}, u32[]{:S(2)}) copy-start(f32[2048,2048]{1,0:T(8,128)S(1)} %get-tuple-element.393) | copy-start | bytes 50331652 | tf_op jit(solution)/shard_map/while
  276.8 5.7 %copy-start = (f32[2048,2048]{1,0:T(8,128)}, f32[2048,2048]{1,0:T(8,128)S(1)}, u32[]{:S(2)}) copy-start(f32[2048,2048]{1,0:T(8,128)S(1)} %get-tuple-element.393) | copy-start | bytes 50331652 | tf_op jit(solution)/shard_map/while
  294.5 5.7 %copy-start = (f32[2048,2048]{1,0:T(8,128)}, f32[2048,2048]{1,0:T(8,128)S(1)}, u32[]{:S(2)}) copy-start(f32[2048,2048]{1,0:T(8,128)S(1)} %get-tuple-element.393) | copy-start | bytes 50331652 | tf_op jit(solution)/shard_map/while
  312.2 5.7 %copy-start = (f32[2048,2048]{1,0:T(8,128)}, f32[2048,2048]{1,0:T(8,128)S(1)}, u32[]{:S(2)}) copy-start(f32[2048,2048]{1,0:T(8,128)S(1)} %get-tuple-element.393) | copy-start | bytes 50331652 | tf_op jit(solution)/shard_map/while
Sparse Core Ops, SparseCore 0:
  9.9 57.7 all-gather.7
  70.2 52.4 all-gather.9
  130.8 53.0 all-gather.5
where the time goes:
time: 354 us; the launch traced here: 353 us
  waiting for transfers between devices  160 us (45%)
  matrix products  103 us (29%)
  other arithmetic  47.6 us (13%)
  blocking collectives  16.4 us (5%)
  between operations  13.3 us (4%)
  local copies, waits for them, and re-layouts  12.9 us (4%)
    all_gather x2, waiting for transfers between devices, piecewise(): finished.append(jax.vmap(apply)(lax.all_gather(share, axis), starts))  106 us
    dot_general x8, matrix products, attend(): jnp.einsum('hgqk,khd->hgqd', weights.astype(jnp.bfloat16), value_part, pr...  65 us
    all_gather x1, waiting for transfers between devices, per_device(): piece = lax.all_gather(key_value_pair, 'grp', axis=0, tiled=True)  52.6 us
    reduce_sum x8, other arithmetic, attend(): totals = totals * factor + jnp.sum(weights, axis=-1)  42.5 us
    dot_general x8, matrix products, attend(): jnp.einsum('qhgd,khd->hgqk', queries, key_part, preferred_element_type=jn...  28.7 us
    all_to_all x1, blocking collectives, per_device(): lax.all_to_all(attended, 'sp', split_axis=0, concat_axis=1, tiled=True)  16.4 us
    dot_general x2, matrix products, project(): return jnp.dot(piece, joined, preferred_element_type=jnp.float32)  9.01 us
  transfers between devices with their start and end apart: 3, of which 3 were waited for; matrix products, arithmetic and copies ran while one was open for 2% of the time, Pallas kernels for 0%

commit v1 on v0

--- a/solution.py
+++ b/solution.py
@@ -1,3 +1,4 @@
+import functools
 import jax
 import jax.numpy as jnp
 from jax import lax
@@ -8,6 +9,17 @@
 BPG = 4
 rope_base = 150000.0
 neg_large = -1e30
+
+
+def begin_the_views(matrix, shard_axis):
+    tile_out = jax.lax.axis_size(shard_axis)
+    y1 = jnp.split(matrix, tile_out, axis=0)
+    t_next = jnp.stack(y1, axis=0)
+    w1 = jax.lax.all_to_all(t_next, axis_name=shard_axis, split_axis=0, concat_axis=0)
+    return jnp.concatenate(w1, axis=1)
+
+
+save_the_squares = functools.partial(begin_the_views, shard_axis="sp")
 
 
 def joined_along(pieces, dim):
@@ -143,7 +155,7 @@
     maxima, totals, mixture = lax.fori_loop(0, turns, visit, initial)
     normed = jnp.transpose(mixture, (2, 0, 1, 3)) / jnp.transpose(totals, (2, 0, 1))[..., None]
     attended = normed.reshape(group_rows, query_cols).astype(jnp.bfloat16)
-    return lax.all_to_all(attended, "sp", split_axis=0, concat_axis=1, tiled=True)
+    return save_the_squares(attended)
 
 
 def solution(mesh):

time: 354 us -> 326 us (0.921)
  matrix products: 103 us -> 78 us
    dot_general x8, matrix products: 65 us -> 40.4 us  [attend(): jnp.einsum('hgqk,khd->hgqd', weights.astype(jnp.bfloat16), value_part, pr...]
    while x26 -> x8, local copies, waits for them, and re-layouts: 3.98 us -> 0.02 us
where the time goes in v1:
time: 326 us; the launch traced here: 325 us
  waiting for transfers between devices  160 us (49%)
  matrix products  78 us (24%)
  other arithmetic  46.8 us (14%)
  blocking collectives  16.4 us (5%)
  between operations  13.4 us (4%)
  local copies, waits for them, and re-layouts  10.1 us (3%)
    all_gather x2, waiting for transfers between devices, piecewise(): finished.append(jax.vmap(apply)(lax.all_gather(share, axis), starts))  106 us
    all_gather x1, waiting for transfers between devices, per_device(): piece = lax.all_gather(key_value_pair, 'grp', axis=0, tiled=True)  52.5 us
    reduce_sum x8, other arithmetic, attend(): totals = totals * factor + jnp.sum(weights, axis=-1)  42.5 us
    dot_general x8, matrix products, attend(): jnp.einsum('hgqk,khd->hgqd', weights.astype(jnp.bfloat16), value_part, pr...  40.4 us
    dot_general x8, matrix products, attend(): jnp.einsum('qhgd,khd->hgqk', queries, key_part, preferred_element_type=jn...  28.6 us
    all_to_all x1, blocking collectives, begin_the_views(): jax.lax.all_to_all(t_next, axis_name=shard_axis, split_axis=0, concat_axi...  16.4 us
    dot_general x2, matrix products, project(): return jnp.dot(piece, joined, preferred_element_type=jnp.float32)  9.02 us
  transfers between devices with their start and end apart: 3, of which 3 were waited for; matrix products, arithmetic and copies ran while one was open for 2% of the time, Pallas kernels for 0%

profile of v1, /device:TPU:1, one launch (start us, length us, event | category | flops | bytes accessed | tf_op | source)
XLA Modules:
  0.0 325.0 jit_solution(11251660683940591663)
XLA Ops:
  6.5 1.8 fusion.62
  8.4 0.7 all-gather.8.cloned.1.call-update
  9.2 1.8 constant_dynamic-slice_fusion.1
  11.0 0.3 copy.26
  11.3 0.3 copy.27
  11.7 0.1 select_reduce_fusion.1
  11.8 55.8 %all-gather.10.cloned.1.call-done = bf16[1024,2880]{1,0:T(8,128)(2,1)} async-done(((bf16[32,2880]{1,0:T(8,128)(2,1)}), bf16[1024,2880]{1,0:T(8,128)(2,1)}) %all-gather.10.cloned.1.call-update) | async-done | bytes 5898256 | tf_op jit(solution)/shard_map/all_gather | solution.py:38
  67.6 4.5 %convolution_bitcast_fusion = f32[32,32,192]{2,1,0:T(8,128)S(1)} fusion(bf16[32,32,2880]{2,1,0:T(8,128)(2,1)} %bitcast.231, bf16[2880,64]{0,1:T(8,128)(2,1)S(1)} %copy.27, bf16[2880,64]{0,1:T(8,128)(2,1)S(1)} %copy.26, bf16[2880,64]{0,1:T(8,128)(2,1)S(1)} %copy-done.1), kind=kOutput, calls=%fused_computation.48 | convolution fusion | flops 1135779840 | bytes 7790592 | tf_op jit(solution)/shard_map/vmap()/dot_general | solution.py:125
  72.2 50.5 %all-gather.8.cloned.1.call-done = bf16[1024,2880]{1,0:T(8,128)(2,1)} async-done(((bf16[32,2880]{1,0:T(8,128)(2,1)}), bf16[1024,2880]{1,0:T(8,128)(2,1)}) %all-gather.8.cloned.1.call-update) | async-done | bytes 5898256 | tf_op jit(solution)/shard_map/all_gather | solution.py:38
  122.6 4.5 %convolution_bitcast_fusion.1 = f32[32,32,192]{2,1,0:T(8,128)S(1)} fusion(bf16[32,32,2880]{2,1,0:T(8,128)(2,1)} %bitcast.232, bf16[2880,64]{0,1:T(8,128)(2,1)S(1)} %copy.27, bf16[2880,64]{0,1:T(8,128)(2,1)S(1)} %copy.26, bf16[2880,64]{0,1:T(8,128)(2,1)S(1)} %copy-done.1), kind=kOutput, calls=%fused_computation.49 | convolution fusion | flops 1135779840 | bytes 7790592 | tf_op jit(solution)/shard_map/vmap()/dot_general | solution.py:125
  127.1 0.2 pad_maximum_fusion
  127.4 0.3 fusion.61
  127.8 0.2 copy.31
  128.0 0.3 copy.32
  128.3 0.3 copy.30
  128.6 1.4 fusion.50
  130.0 0.9 pad_maximum_fusion.1
  130.9 0.7 dynamic_slice.20
  131.6 52.5 %all-gather.6.cloned.1.call-done = bf16[16384,128]{0,1:T(8,128)(2,1)} async-done(((bf16[2048,128]{0,1:T(8,128)(2,1)}), bf16[16384,128]{0,1:T(8,128)(2,1)}) %all-gather.6.cloned.1.call-update) | async-done | bytes 4194320 | tf_op jit(solution)/shard_map/all_gather | solution.py:143
  184.1 0.7 broadcast_in_dim.68
  184.8 113.8 %while.21 = (s32[]{:T(128)}, f32[1,1,2048]{2,1,0:T(1,128)S(1)}, f32[1,1,2048]{2,1,0:T(1,128)S(1)}, f32[1,1,2048,64]{2,3,1,0:T(8,128)S(1)}, s32[32]{0:T(128)S(1)}...) while((s32[]{:T(128)}, f32[1,1,2048]{2,1,0:T(1,128)S(1)}, ...), condition=%wide.region_5.6_spmd.clone, body=%wide.region_1.5_spmd.clone.sunk | while | flops 1141592064 | bytes 52388188 | solution.py:155
  184.9 0.1 select_reduce_fusion.3
  185.0 3.6 %fusion.75 = (f32[2048]{0:T(1024)S(1)}, f32[2048,2048]{1,0:T(8,128)S(1)}) fusion(s32[2048]{0:T(1024)S(1)} %get-tuple-element.411, s32[2048]{0:T(1024)S(1)} %fusion.74, bf16[2048,1,1,64]{0,3,2,1:T(8,128)(2,1)S(1)} %get-tuple-element.413, bf16[16384,128]{0,1:T(8,128)(2,1)} %get-tuple-element.412, s32[]{:T(128)S(6)} %select_n.248), kind=kOutput, calls=%fused_computation.2.clone.1 | convolution fusion | flops 553646080 | bytes 17326084 | tf_op jit(solution)/shard_map/while/body/eval_jaxpr/qhgd,khd->hgqk/dot_general | solution.py:87
  188.7 5.3 %fusion.76 = f32[2048]{0:T(1024)S(1)} fusion(f32[2048,2048]{1,0:T(8,128)S(1)} %get-tuple-element.377, f32[2048]{0:T(1024)S(1)} %bitcast.221, s32[2048]{0:T(1024)S(1)} %get-tuple-element.411, s32[2048]{0:T(1024)S(1)} %fusion.74), kind=kLoop, calls=%fused_computation.4.clone.1 | loop fusion | flops 25163776 | bytes 16809984 | tf_op jit(solution)/shard_map/while/body/eval_jaxpr/reduce_sum | solution.py:95
  194.0 5.0 %fusion.78 = f32[1,1,2048,64]{2,3,1,0:T(8,128)S(1)} fusion(f32[2048,2048]{1,0:T(8,128)S(1)} %get-tuple-element.377, f32[2048]{0:T(1024)S(1)} %bitcast.222, s32[2048]{0:T(1024)S(1)} %get-tuple-element.411, s32[2048]{0:T(1024)S(1)} %fusion.74, f32[1,1,2048,64]{2,3,1,0:T(8,128)S(1)} %get-tuple-element.396, bf16[16384,128]{0,1:T(8,128)(2,1)} %get-tuple-element.412, ...), kind=kOutput, calls=%fused_computation.8.clone.1 | convolution fusion | flops 562429952 | bytes 18120712 | tf_op jit(solution)/shard_map/while/body/eval_jaxpr/hgqk,khd->hgqd/dot_general | solution.py:96
  199.1 0.1 select_reduce_fusion.3
  199.3 3.6 %fusion.75 = (f32[2048]{0:T(1024)S(1)}, f32[2048,2048]{1,0:T(8,128)S(1)}) fusion(s32[2048]{0:T(1024)S(1)} %get-tuple-element.411, s32[2048]{0:T(1024)S(1)} %fusion.74, bf16[2048,1,1,64]{0,3,2,1:T(8,128)(2,1)S(1)} %get-tuple-element.413, bf16[16384,128]{0,1:T(8,128)(2,1)} %get-tuple-element.412, s32[]{:T(128)S(6)} %select_n.248), kind=kOutput, calls=%fused_computation.2.clone.1 | convolution fusion | flops 553646080 | bytes 17326084 | tf_op jit(solution)/shard_map/while/body/eval_jaxpr/qhgd,khd->hgqk/dot_general | solution.py:87
  202.9 5.3 %fusion.76 = f32[2048]{0:T(1024)S(1)} fusion(f32[2048,2048]{1,0:T(8,128)S(1)} %get-tuple-element.377, f32[2048]{0:T(1024)S(1)} %bitcast.221, s32[2048]{0:T(1024)S(1)} %get-tuple-element.411, s32[2048]{0:T(1024)S(1)} %fusion.74), kind=kLoop, calls=%fused_computation.4.clone.1 | loop fusion | flops 25163776 | bytes 16809984 | tf_op jit(solution)/shard_map/while/body/eval_jaxpr/reduce_sum | solution.py:95
  208.2 5.0 %fusion.78 = f32[1,1,2048,64]{2,3,1,0:T(8,128)S(1)} fusion(f32[2048,2048]{1,0:T(8,128)S(1)} %get-tuple-element.377, f32[2048]{0:T(1024)S(1)} %bitcast.222, s32[2048]{0:T(1024)S(1)} %get-tuple-element.411, s32[2048]{0:T(1024)S(1)} %fusion.74, f32[1,1,2048,64]{2,3,1,0:T(8,128)S(1)} %get-tuple-element.396, bf16[16384,128]{0,1:T(8,128)(2,1)} %get-tuple-element.412, ...), kind=kOutput, calls=%fused_computation.8.clone.1 | convolution fusion | flops 562429952 | bytes 18120712 | tf_op jit(solution)/shard_map/while/body/eval_jaxpr/hgqk,khd->hgqd/dot_general | solution.py:96
  213.3 0.1 select_reduce_fusion.3
  213.5 3.6 %fusion.75 = (f32[2048]{0:T(1024)S(1)}, f32[2048,2048]{1,0:T(8,128)S(1)}) fusion(s32[2048]{0:T(1024)S(1)} %get-tuple-element.411, s32[2048]{0:T(1024)S(1)} %fusion.74, bf16[2048,1,1,64]{0,3,2,1:T(8,128)(2,1)S(1)} %get-tuple-element.413, bf16[16384,128]{0,1:T(8,128)(2,1)} %get-tuple-element.412, s32[]{:T(128)S(6)} %select_n.248), kind=kOutput, calls=%fused_computation.2.clone.1 | convolution fusion | flops 553646080 | bytes 17326084 | tf_op jit(solution)/shard_map/while/body/eval_jaxpr/qhgd,khd->hgqk/dot_general | solution.py:87
  217.1 5.3 %fusion.76 = f32[2048]{0:T(1024)S(1)} fusion(f32[2048,2048]{1,0:T(8,128)S(1)} %get-tuple-element.377, f32[2048]{0:T(1024)S(1)} %bitcast.221, s32[2048]{0:T(1024)S(1)} %get-tuple-element.411, s32[2048]{0:T(1024)S(1)} %fusion.74), kind=kLoop, calls=%fused_computation.4.clone.1 | loop fusion | flops 25163776 | bytes 16809984 | tf_op jit(solution)/shard_map/while/body/eval_jaxpr/reduce_sum | solution.py:95
  222.5 5.0 %fusion.78 = f32[1,1,2048,64]{2,3,1,0:T(8,128)S(1)} fusion(f32[2048,2048]{1,0:T(8,128)S(1)} %get-tuple-element.377, f32[2048]{0:T(1024)S(1)} %bitcast.222, s32[2048]{0:T(1024)S(1)} %get-tuple-element.411, s32[2048]{0:T(1024)S(1)} %fusion.74, f32[1,1,2048,64]{2,3,1,0:T(8,128)S(1)} %get-tuple-element.396, bf16[16384,128]{0,1:T(8,128)(2,1)} %get-tuple-element.412, ...), kind=kOutput, calls=%fused_computation.8.clone.1 | convolution fusion | flops 562429952 | bytes 18120712 | tf_op jit(solution)/shard_map/while/body/eval_jaxpr/hgqk,khd->hgqd/dot_general | solution.py:96
  227.6 0.1 select_reduce_fusion.3
  227.7 3.6 %fusion.75 = (f32[2048]{0:T(1024)S(1)}, f32[2048,2048]{1,0:T(8,128)S(1)}) fusion(s32[2048]{0:T(1024)S(1)} %get-tuple-element.411, s32[2048]{0:T(1024)S(1)} %fusion.74, bf16[2048,1,1,64]{0,3,2,1:T(8,128)(2,1)S(1)} %get-tuple-element.413, bf16[16384,128]{0,1:T(8,128)(2,1)} %get-tuple-element.412, s32[]{:T(128)S(6)} %select_n.248), kind=kOutput, calls=%fused_computation.2.clone.1 | convolution fusion | flops 553646080 | bytes 17326084 | tf_op jit(solution)/shard_map/while/body/eval_jaxpr/qhgd,khd->hgqk/dot_general | solution.py:87
  231.3 5.3 %fusion.76 = f32[2048]{0:T(1024)S(1)} fusion(f32[2048,2048]{1,0:T(8,128)S(1)} %get-tuple-element.377, f32[2048]{0:T(1024)S(1)} %bitcast.221, s32[2048]{0:T(1024)S(1)} %get-tuple-element.411, s32[2048]{0:T(1024)S(1)} %fusion.74), kind=kLoop, calls=%fused_computation.4.clone.1 | loop fusion | flops 25163776 | bytes 16809984 | tf_op jit(solution)/shard_map/while/body/eval_jaxpr/reduce_sum | solution.py:95
  236.7 5.0 %fusion.78 = f32[1,1,2048,64]{2,3,1,0:T(8,128)S(1)} fusion(f32[2048,2048]{1,0:T(8,128)S(1)} %get-tuple-element.377, f32[2048]{0:T(1024)S(1)} %bitcast.222, s32[2048]{0:T(1024)S(1)} %get-tuple-element.411, s32[2048]{0:T(1024)S(1)} %fusion.74, f32[1,1,2048,64]{2,3,1,0:T(8,128)S(1)} %get-tuple-element.396, bf16[16384,128]{0,1:T(8,128)(2,1)} %get-tuple-element.412, ...), kind=kOutput, calls=%fused_computation.8.clone.1 | convolution fusion | flops 562429952 | bytes 18120712 | tf_op jit(solution)/shard_map/while/body/eval_jaxpr/hgqk,khd->hgqd/dot_general | solution.py:96
  241.8 0.1 select_reduce_fusion.3
  241.9 3.6 %fusion.75 = (f32[2048]{0:T(1024)S(1)}, f32[2048,2048]{1,0:T(8,128)S(1)}) fusion(s32[2048]{0:T(1024)S(1)} %get-tuple-element.411, s32[2048]{0:T(1024)S(1)} %fusion.74, bf16[2048,1,1,64]{0,3,2,1:T(8,128)(2,1)S(1)} %get-tuple-element.413, bf16[16384,128]{0,1:T(8,128)(2,1)} %get-tuple-element.412, s32[]{:T(128)S(6)} %select_n.248), kind=kOutput, calls=%fused_computation.2.clone.1 | convolution fusion | flops 553646080 | bytes 17326084 | tf_op jit(solution)/shard_map/while/body/eval_jaxpr/qhgd,khd->hgqk/dot_general | solution.py:87
  245.5 5.3 %fusion.76 = f32[2048]{0:T(1024)S(1)} fusion(f32[2048,2048]{1,0:T(8,128)S(1)} %get-tuple-element.377, f32[2048]{0:T(1024)S(1)} %bitcast.221, s32[2048]{0:T(1024)S(1)} %get-tuple-element.411, s32[2048]{0:T(1024)S(1)} %fusion.74), kind=kLoop, calls=%fused_computation.4.clone.1 | loop fusion | flops 25163776 | bytes 16809984 | tf_op jit(solution)/shard_map/while/body/eval_jaxpr/reduce_sum | solution.py:95
  250.9 5.0 %fusion.78 = f32[1,1,2048,64]{2,3,1,0:T(8,128)S(1)} fusion(f32[2048,2048]{1,0:T(8,128)S(1)} %get-tuple-element.377, f32[2048]{0:T(1024)S(1)} %bitcast.222, s32[2048]{0:T(1024)S(1)} %get-tuple-element.411, s32[2048]{0:T(1024)S(1)} %fusion.74, f32[1,1,2048,64]{2,3,1,0:T(8,128)S(1)} %get-tuple-element.396, bf16[16384,128]{0,1:T(8,128)(2,1)} %get-tuple-element.412, ...), kind=kOutput, calls=%fused_computation.8.clone.1 | convolution fusion | flops 562429952 | bytes 18120712 | tf_op jit(solution)/shard_map/while/body/eval_jaxpr/hgqk,khd->hgqd/dot_general | solution.py:96
  256.0 0.1 select_reduce_fusion.3
  256.2 3.6 %fusion.75 = (f32[2048]{0:T(1024)S(1)}, f32[2048,2048]{1,0:T(8,128)S(1)}) fusion(s32[2048]{0:T(1024)S(1)} %get-tuple-element.411, s32[2048]{0:T(1024)S(1)} %fusion.74, bf16[2048,1,1,64]{0,3,2,1:T(8,128)(2,1)S(1)} %get-tuple-element.413, bf16[16384,128]{0,1:T(8,128)(2,1)} %get-tuple-element.412, s32[]{:T(128)S(6)} %select_n.248), kind=kOutput, calls=%fused_computation.2.clone.1 | convolution fusion | flops 553646080 | bytes 17326084 | tf_op jit(solution)/shard_map/while/body/eval_jaxpr/qhgd,khd->hgqk/dot_general | solution.py:87
  259.8 5.3 %fusion.76 = f32[2048]{0:T(1024)S(1)} fusion(f32[2048,2048]{1,0:T(8,128)S(1)} %get-tuple-element.377, f32[2048]{0:T(1024)S(1)} %bitcast.221, s32[2048]{0:T(1024)S(1)} %get-tuple-element.411, s32[2048]{0:T(1024)S(1)} %fusion.74), kind=kLoop, calls=%fused_computation.4.clone.1 | loop fusion | flops 25163776 | bytes 16809984 | tf_op jit(solution)/shard_map/while/body/eval_jaxpr/reduce_sum | solution.py:95
  265.1 5.0 %fusion.78 = f32[1,1,2048,64]{2,3,1,0:T(8,128)S(1)} fusion(f32[2048,2048]{1,0:T(8,128)S(1)} %get-tuple-element.377, f32[2048]{0:T(1024)S(1)} %bitcast.222, s32[2048]{0:T(1024)S(1)} %get-tuple-element.411, s32[2048]{0:T(1024)S(1)} %fusion.74, f32[1,1,2048,64]{2,3,1,0:T(8,128)S(1)} %get-tuple-element.396, bf16[16384,128]{0,1:T(8,128)(2,1)} %get-tuple-element.412, ...), kind=kOutput, calls=%fused_computation.8.clone.1 | convolution fusion | flops 562429952 | bytes 18120712 | tf_op jit(solution)/shard_map/while/body/eval_jaxpr/hgqk,khd->hgqd/dot_general | solution.py:96
  270.2 0.1 select_reduce_fusion.3
  270.4 3.6 %fusion.75 = (f32[2048]{0:T(1024)S(1)}, f32[2048,2048]{1,0:T(8,128)S(1)}) fusion(s32[2048]{0:T(1024)S(1)} %get-tuple-element.411, s32[2048]{0:T(1024)S(1)} %fusion.74, bf16[2048,1,1,64]{0,3,2,1:T(8,128)(2,1)S(1)} %get-tuple-element.413, bf16[16384,128]{0,1:T(8,128)(2,1)} %get-tuple-element.412, s32[]{:T(128)S(6)} %select_n.248), kind=kOutput, calls=%fused_computation.2.clone.1 | convolution fusion | flops 553646080 | bytes 17326084 | tf_op jit(solution)/shard_map/while/body/eval_jaxpr/qhgd,khd->hgqk/dot_general | solution.py:87
  274.0 5.3 %fusion.76 = f32[2048]{0:T(1024)S(1)} fusion(f32[2048,2048]{1,0:T(8,128)S(1)} %get-tuple-element.377, f32[2048]{0:T(1024)S(1)} %bitcast.221, s32[2048]{0:T(1024)S(1)} %get-tuple-element.411, s32[2048]{0:T(1024)S(1)} %fusion.74), kind=kLoop, calls=%fused_computation.4.clone.1 | loop fusion | flops 25163776 | bytes 16809984 | tf_op jit(solution)/shard_map/while/body/eval_jaxpr/reduce_sum | solution.py:95
  279.3 5.0 %fusion.78 = f32[1,1,2048,64]{2,3,1,0:T(8,128)S(1)} fusion(f32[2048,2048]{1,0:T(8,128)S(1)} %get-tuple-element.377, f32[2048]{0:T(1024)S(1)} %bitcast.222, s32[2048]{0:T(1024)S(1)} %get-tuple-element.411, s32[2048]{0:T(1024)S(1)} %fusion.74, f32[1,1,2048,64]{2,3,1,0:T(8,128)S(1)} %get-tuple-element.396, bf16[16384,128]{0,1:T(8,128)(2,1)} %get-tuple-element.412, ...), kind=kOutput, calls=%fused_computation.8.clone.1 | convolution fusion | flops 562429952 | bytes 18120712 | tf_op jit(solution)/shard_map/while/body/eval_jaxpr/hgqk,khd->hgqd/dot_general | solution.py:96
  284.5 0.1 select_reduce_fusion.3
  284.6 3.6 %fusion.75 = (f32[2048]{0:T(1024)S(1)}, f32[2048,2048]{1,0:T(8,128)S(1)}) fusion(s32[2048]{0:T(1024)S(1)} %get-tuple-element.411, s32[2048]{0:T(1024)S(1)} %fusion.74, bf16[2048,1,1,64]{0,3,2,1:T(8,128)(2,1)S(1)} %get-tuple-element.413, bf16[16384,128]{0,1:T(8,128)(2,1)} %get-tuple-element.412, s32[]{:T(128)S(6)} %select_n.248), kind=kOutput, calls=%fused_computation.2.clone.1 | convolution fusion | flops 553646080 | bytes 17326084 | tf_op jit(solution)/shard_map/while/body/eval_jaxpr/qhgd,khd->hgqk/dot_general | solution.py:87
  288.2 5.3 %fusion.76 = f32[2048]{0:T(1024)S(1)} fusion(f32[2048,2048]{1,0:T(8,128)S(1)} %get-tuple-element.377, f32[2048]{0:T(1024)S(1)} %bitcast.221, s32[2048]{0:T(1024)S(1)} %get-tuple-element.411, s32[2048]{0:T(1024)S(1)} %fusion.74), kind=kLoop, calls=%fused_computation.4.clone.1 | loop fusion | flops 25163776 | bytes 16809984 | tf_op jit(solution)/shard_map/while/body/eval_jaxpr/reduce_sum | solution.py:95
  293.6 5.0 %fusion.78 = f32[1,1,2048,64]{2,3,1,0:T(8,128)S(1)} fusion(f32[2048,2048]{1,0:T(8,128)S(1)} %get-tuple-element.377, f32[2048]{0:T(1024)S(1)} %bitcast.222, s32[2048]{0:T(1024)S(1)} %get-tuple-element.411, s32[2048]{0:T(1024)S(1)} %fusion.74, f32[1,1,2048,64]{2,3,1,0:T(8,128)S(1)} %get-tuple-element.396, bf16[16384,128]{0,1:T(8,128)(2,1)} %get-tuple-element.412, ...), kind=kOutput, calls=%fused_computation.8.clone.1 | convolution fusion | flops 562429952 | bytes 18120712 | tf_op jit(solution)/shard_map/while/body/eval_jaxpr/hgqk,khd->hgqd/dot_general | solution.py:96
  298.7 0.1 constant_dynamic-update-slice_fusion.30
  298.8 0.1 constant_dynamic-update-slice_fusion.28
  299.0 0.1 constant_dynamic-update-slice_fusion.24
  299.1 0.1 constant_dynamic-update-slice_fusion.22
  299.2 0.1 constant_dynamic-update-slice_fusion.20
  299.3 0.1 constant_dynamic-update-slice_fusion.18
  299.6 0.1 constant_dynamic-update-slice_fusion.14
  300.4 0.4 reshape.431
  300.8 16.4 %all_to_all.5 = bf16[32,2,2048]{2,1,0:T(2,128)(2,1)S(1)} all-to-all(bf16[32,2,2048]{2,1,0:T(2,128)(2,1)S(1)} %reshape.431), channel_id=1, replica_groups=mesh['grp'=8,'sp'=32] {'sp'}, dimensions={0} | all-to-all | bytes 524288 | tf_op jit(solution)/shard_map/all_to_all | solution.py:18
  317.2 0.4 reshape.432
  317.5 0.9 copy.24
  (85 shorter events, 2.1 us)
Async XLA Ops:
  6.5 5.1 %copy-start = (s32[32]{0:T(128)S(1)}, s32[32]{0:T(128)}, u32[]{:S(2)}) copy-start(s32[32]{0:T(128)} %param.10) | copy-start | bytes 388
  6.5 61.1 %copy-start.1 = (bf16[2880,64]{0,1:T(8,128)(2,1)S(1)}, bf16[2880,64]{0,1:T(8,128)(2,1)}, u32[]{:S(2)}) copy-start(bf16[2880,64]{0,1:T(8,128)(2,1)} %param.8) | copy-start | bytes 1105924
  6.5 61.1 %all-gather.10.cloned.1.call-start = ((), (), s32[]{:S(2)}) async-start(), calls=%async_computation.3 | async-start | bytes 6217728 | tf_op jit(solution)/shard_map/all_gather | solution.py:38
  8.4 114.2 %all-gather.8.cloned.1.call-start = ((), (), s32[]{:S(2)}) async-start(), calls=%async_computation.2 | async-start | bytes 6217728 | tf_op jit(solution)/shard_map/all_gather | solution.py:38
  9.1 175.0 %all-gather.6.cloned.1.call-start = ((), (), s32[]{:S(2)}) async-start(), calls=%async_computation.1 | async-start | bytes 4718592 | tf_op jit(solution)/shard_map/all_gather | solution.py:143
  127.4 3.5 %copy-start.2 = (f32[32]{0:T(128)S(1)}, f32[32]{0:T(128)}, u32[]{:S(2)}) copy-start(f32[32]{0:T(128)} %param.11) | copy-start | bytes 388
Sparse Core Ops, SparseCore 0:
  9.9 57.7 all-gather.9
  70.2 52.4 all-gather.7
  131.0 53.0 all-gather.5
